TPU v7x, 128 devices: a whole 4x4x4 slice. The times are simulated.
128 devices in a mesh: tiles: 32 (over x, y, core), reps: 4 (over z).
Axes of the slice: x: 4, y: 4, z: 4, core: 2. Of those that a mesh axis runs over, the one named last changes fastest.
Arguments:
- tiles_w: bfloat16 [4096, 128, 128], P('tiles'), may hold values from 0.0001 to 4
- tile_worker: int32 [4096], P('tiles'), may hold values from 0 to 15
- tile_owner: int32 [4096], P('tiles'), may hold values from 0 to 31
- owner_block: int32 [32, 32], P('tiles'), may hold values from 0 to 1
- worker_base: float32 [65536], P('tiles'), may hold values from -6 to 6
- worker_noise: float32 [65536], P('tiles'), may hold values from 0.2 to 1.5
- worker_cluster: int32 [65536], P('tiles'), may hold values from 0 to 255
- firm_base: float32 [8192], P('tiles'), may hold values from -6 to 6
- firm_noise: float32 [8192], P('tiles'), may hold values from 0.2 to 1.5
- firm_cluster: int32 [8192], P('tiles'), may hold values from 0 to 255
- signs: int32 [256, 256], P('reps'), may hold values from 0 to 1
- covariates: float32 [8192, 512], P('tiles'), may hold values from -0.0625 to 0.0625
- whitening: float32 [512, 512], replicated, may hold values from -0.25 to 0.25
Outputs:
- worker_effect: float32 [256, 65536], P('reps', 'tiles')
- firm_effect: float32 [256, 8192], P('reps', 'tiles')
- coefficients: float32 [256, 512], P('reps')
- covariance: float32 [512, 512], P('tiles')
Inputs may be any that keep to these rules, and one draw needn't show every extreme that they name: `tile_worker`: local worker block of each tile. `tile_owner`: owner of each tile's firm block. `owner_block`: firm block among the owner's 2 blocks. `signs`: a bit that gives the sign 2 b - 1.
All inputs are finite; a program needn't handle non-finite values.
Results may differ from a plain program's by a relative error of at most 0.0023.
Values may be sent and summed in bfloat16 or wider, within the bound.
No kernel may reach another device: no remote copies, remote signals or barrier semaphores. Data moves between devices by JAX's collectives and lax.ppermute only.
A program may use at most 64 MiB of HBM per device.

v0:
```python
import jax
import jax.numpy as jnp
from jax import lax
from jax.sharding import PartitionSpec as P

WORK_BLOCKS = 16
FIRM_BLOCKS = 2
SWEEPS = 6
spectral_bound = 0.8


def chebyshev_weights(sweep_count):
    weights = [1.0]
    weights.append(1.0 / (1.0 - 0.5 * spectral_bound * spectral_bound))
    while len(weights) < sweep_count:
        weights.append(1.0 / (1.0 - 0.25 * spectral_bound * spectral_bound * weights[-1]))
    return weights


def one_hot_rows(indices, row_count):
    return (indices[None, :] == jnp.arange(row_count, dtype=jnp.int32)[:, None]).astype(jnp.float32)


def wild_outcome(base_value, noise_scale, cluster, flip_table):
    clusters_hot = (
        cluster[None, :] == jnp.arange(flip_table.shape[1], dtype=jnp.int32)[:, None]
    ).astype(jnp.bfloat16)
    flip_values = jnp.dot(flip_table, clusters_hot, preferred_element_type=jnp.float32)
    return base_value[None, :] + noise_scale[None, :] * flip_values


def body(
    tiles_w,
    tile_worker,
    tile_owner,
    owner_block,
    worker_base,
    worker_noise,
    worker_cluster,
    firm_base,
    firm_noise,
    firm_cluster,
    signs,
    covariates,
    whitening,
):
    highest = lax.Precision.HIGHEST
    owners_count = lax.axis_size("tiles")
    tile_cells = tiles_w.shape[1]
    replicas_here = signs.shape[0]
    flip_table = (2 * signs - 1).astype(jnp.bfloat16)
    worker_outcome = wild_outcome(worker_base, worker_noise, worker_cluster, flip_table).reshape(
        replicas_here, WORK_BLOCKS, tile_cells
    )
    firm_outcome = wild_outcome(firm_base, firm_noise, firm_cluster, flip_table).reshape(
        replicas_here, FIRM_BLOCKS, tile_cells
    )
    row_mass = jnp.sum(tiles_w, axis=2, dtype=jnp.float32)
    col_mass = jnp.sum(tiles_w, axis=1, dtype=jnp.float32)
    worker_hot = one_hot_rows(tile_worker, WORK_BLOCKS)
    worker_scale = 1.0 + jnp.einsum("bt,tw->bw", worker_hot, row_mass, precision=highest)
    owner_hot = one_hot_rows(tile_owner, owners_count)
    my_blocks = owner_block[0]
    tile_block = tile_owner * FIRM_BLOCKS + jnp.sum(
        jnp.where(owner_hot > 0, my_blocks[:, None], 0), axis=0
    )
    dense_hot = one_hot_rows(tile_block, owners_count * FIRM_BLOCKS)
    firm_mass = lax.psum_scatter(
        jnp.einsum("nt,tf->nf", dense_hot, col_mass, precision=highest),
        "tiles",
        scatter_dimension=0,
        tiled=True,
    )
    firm_scale = 1.0 + firm_mass
    omegas = chebyshev_weights(SWEEPS)
    firm_older = jnp.zeros((replicas_here, FIRM_BLOCKS, tile_cells), jnp.float32)
    firm_newer = firm_older
    firm_now = firm_older
    worker_now = worker_outcome
    tile_firm = None
    for sweep_index in range(SWEEPS):
        if sweep_index == 0:
            worker_now = worker_outcome
        else:
            pulled = jnp.einsum(
                "twf,rtf->rtw", tiles_w, tile_firm, preferred_element_type=jnp.float32
            )
            worker_sum = jnp.einsum("bt,rtw->rbw", worker_hot, pulled, precision=highest)
            worker_now = worker_outcome - worker_sum / worker_scale[None]
        worker_round = worker_now.astype(jnp.bfloat16)
        tile_values = jnp.take(worker_round, tile_worker, axis=1)
        pushed = jnp.einsum(
            "twf,rtw->rtf", tiles_w, tile_values, preferred_element_type=jnp.float32
        )
        firm_sum = lax.psum_scatter(
            jnp.einsum("nt,rtf->rnf", dense_hot, pushed, precision=highest),
            "tiles",
            scatter_dimension=1,
            tiled=True,
        )
        firm_target = firm_outcome - firm_sum / firm_scale[None]
        firm_now = firm_older + omegas[sweep_index] * (firm_target - firm_older)
        firm_older, firm_newer = (firm_newer, firm_now)
        if sweep_index + 1 < SWEEPS:
            firm_round = firm_now.astype(jnp.bfloat16)
            every_firm = lax.all_gather(firm_round, "tiles", axis=1, tiled=True)
            tile_firm = jnp.take(every_firm, tile_block, axis=1)
    worker_effect = worker_now.reshape(replicas_here, WORK_BLOCKS * tile_cells)
    firm_flat = firm_now.reshape(replicas_here, FIRM_BLOCKS * tile_cells)
    mixing = jnp.dot(covariates, whitening.T, precision=highest)
    local_term = jnp.dot(firm_flat, mixing, precision=highest)
    summed = lax.psum(local_term, "tiles")
    share_rows = summed.shape[1] // owners_count
    own_columns = lax.dynamic_slice_in_dim(
        summed, lax.axis_index("tiles") * share_rows, share_rows, 1
    )
    moment = jnp.dot(own_columns.T, summed, precision=highest)
    covariance = lax.psum(moment, "reps") / (replicas_here * lax.axis_size("reps"))
    return (worker_effect, firm_flat, summed, covariance)


def solution(mesh):
    placed = (
        P("tiles", None, None),
        P("tiles"),
        P("tiles"),
        P("tiles", None),
        P("tiles"),
        P("tiles"),
        P("tiles"),
        P("tiles"),
        P("tiles"),
        P("tiles"),
        P("reps", None),
        P("tiles", None),
        P(),
    )
    return jax.shard_map(
        body,
        mesh=mesh,
        in_specs=placed,
        out_specs=(P("reps", "tiles"), P("reps", "tiles"), P("reps", None), P("tiles", None)),
        check_vma=False,
    )
```

profile of v0, /device:TPU:6, one launch (start us, length us, event | category | flops | bytes accessed | tf_op | source)
XLA Modules:
  0.0 1033.3 jit_solution(7390925900868006559)
XLA Ops:
  16.6 4.2 fusion.56
  28.9 109.8 %all-reduce = f32[64,128]{1,0:T(8,128)S(1)} all-reduce(f32[64,128]{1,0:T(8,128)S(1)} %fusion.164), channel_id=3, replica_groups=mesh['tiles'=32,'reps'=4] {'tiles'}, use_global_device_ids=true, to_apply=%region_3.0.clone | all-reduce | flops 8192 | bytes 65536
  140.8 57.8 %all-gather.6.cloned.1.call-done = bf16[64,64,128]{2,0,1:T(8,128)(2,1)} async-done(((bf16[64,2,128]{2,0,1:T(8,128)(2,1)}), bf16[64,64,128]{2,0,1:T(8,128)(2,1)}) %all-gather.6.cloned.1.call-update) | async-done | bytes 1048592 | tf_op jit(solution)/shard_map/all_gather | solution.py:106
  202.0 5.8 convolution_bitcast_fusion.9
  217.9 4.2 fusion.59
  225.1 78.4 %reduce-scatter.9.cloned.1.call-done = f32[64,2,128]{2,0,1:T(8,128)} async-done(((f32[64,64,128]{2,0,1:T(8,128)}), f32[64,2,128]{2,0,1:T(8,128)}) %reduce-scatter.9.cloned.1.call-update) | async-done | bytes 65552 | tf_op jit(solution)/shard_map/reduce_scatter | solution.py:95
  305.0 43.0 %all-gather.8.cloned.1.call-done = bf16[64,64,128]{2,0,1:T(8,128)(2,1)} async-done(((bf16[64,2,128]{2,0,1:T(8,128)(2,1)}), bf16[64,64,128]{2,0,1:T(8,128)(2,1)}) %all-gather.8.cloned.1.call-update) | async-done | bytes 1048592 | tf_op jit(solution)/shard_map/all_gather | solution.py:106
  351.3 5.8 convolution_bitcast_fusion.7
  367.3 4.2 fusion.62
  374.2 78.4 %reduce-scatter.11.cloned.1.call-done = f32[64,2,128]{2,0,1:T(8,128)} async-done(((f32[64,64,128]{2,0,1:T(8,128)}), f32[64,2,128]{2,0,1:T(8,128)}) %reduce-scatter.11.cloned.1.call-update) | async-done | bytes 65552 | tf_op jit(solution)/shard_map/reduce_scatter | solution.py:95
  454.2 43.0 %all-gather.10.cloned.1.call-done = bf16[64,64,128]{2,0,1:T(8,128)(2,1)} async-done(((bf16[64,2,128]{2,0,1:T(8,128)(2,1)}), bf16[64,64,128]{2,0,1:T(8,128)(2,1)}) %all-gather.10.cloned.1.call-update) | async-done | bytes 1048592 | tf_op jit(solution)/shard_map/all_gather | solution.py:106
  500.5 5.7 convolution_bitcast_fusion.5
  516.4 4.2 fusion.65
  523.6 78.4 %reduce-scatter.13.cloned.1.call-done = f32[64,2,128]{2,0,1:T(8,128)} async-done(((f32[64,64,128]{2,0,1:T(8,128)}), f32[64,2,128]{2,0,1:T(8,128)}) %reduce-scatter.13.cloned.1.call-update) | async-done | bytes 65552 | tf_op jit(solution)/shard_map/reduce_scatter | solution.py:95
  603.5 43.1 %all-gather.12.cloned.1.call-done = bf16[64,64,128]{2,0,1:T(8,128)(2,1)} async-done(((bf16[64,2,128]{2,0,1:T(8,128)(2,1)}), bf16[64,64,128]{2,0,1:T(8,128)(2,1)}) %all-gather.12.cloned.1.call-update) | async-done | bytes 1048592 | tf_op jit(solution)/shard_map/all_gather | solution.py:106
  650.0 5.8 convolution_bitcast_fusion.3
  665.9 4.2 fusion.68
  672.9 78.4 %reduce-scatter.15.cloned.1.call-done = f32[64,2,128]{2,0,1:T(8,128)} async-done(((f32[64,64,128]{2,0,1:T(8,128)}), f32[64,2,128]{2,0,1:T(8,128)}) %reduce-scatter.15.cloned.1.call-update) | async-done | bytes 65552 | tf_op jit(solution)/shard_map/reduce_scatter | solution.py:95
  752.8 43.0 %all-gather.14.cloned.1.call-done = bf16[64,64,128]{2,0,1:T(8,128)(2,1)} async-done(((bf16[64,2,128]{2,0,1:T(8,128)(2,1)}), bf16[64,64,128]{2,0,1:T(8,128)(2,1)}) %all-gather.14.cloned.1.call-update) | async-done | bytes 1048592 | tf_op jit(solution)/shard_map/all_gather | solution.py:106
  799.1 5.8 convolution_bitcast_fusion.1
  815.1 4.2 fusion.71
  824.1 76.3 %reduce-scatter.17.cloned.1.call-done = f32[64,2,128]{2,0,1:T(8,128)} async-done(((f32[64,64,128]{2,0,1:T(8,128)}), f32[64,2,128]{2,0,1:T(8,128)}) %reduce-scatter.17.cloned.1.call-update) | async-done | bytes 65552 | tf_op jit(solution)/shard_map/reduce_scatter | solution.py:95
  903.4 102.1 %all-reduce.3.cloned.1.call-done = f32[64,512]{1,0:T(8,128)} async-done(((f32[64,512]{1,0:T(8,128)}), f32[64,512]{1,0:T(8,128)}) %all-reduce.3.cloned.1.call-update) | async-done | bytes 131088 | tf_op jit(solution)/shard_map/psum | solution.py:112
  1006.8 17.3 %psum.15 = f32[16,512]{1,0:T(8,128)S(1)} all-reduce(f32[16,512]{1,0:T(8,128)S(1)} %fusion.162), channel_id=1, replica_groups=mesh['tiles'=32,'reps'=4] {'reps'}, use_global_device_ids=true, to_apply=%region_11.14 | all-reduce | flops 8192 | bytes 65536 | tf_op jit(solution)/shard_map/psum | solution.py:118
  (113 shorter events, 115.5 us)
Async XLA Ops:
  7.2 814.9 %copy-start = (f32[512,512]{1,0:T(8,128)S(1)}, f32[512,512]{1,0:T(8,128)}, u32[]{:S(2)}) copy-start(f32[512,512]{1,0:T(8,128)} %param.29) | copy-start | bytes 3145732
  7.2 3.1 copy-start.11
  7.2 3.1 copy-start.6
  7.2 131.7 %reduce-scatter.7.cloned.1.call-start = ((), (), s32[]{:S(2)}) async-start(), calls=%async_computation.6 | async-start | bytes 2162688 | tf_op jit(solution)/shard_map/reduce_scatter | solution.py:95
  23.4 175.2 %all-gather.6.cloned.1.call-start = ((), (), s32[]{:S(2)}) async-start(), calls=%async_computation.7 | async-start | bytes 1081344 | tf_op jit(solution)/shard_map/all_gather | solution.py:106
  25.2 113.4 %copy-start.7 = (s32[64,256]{1,0:T(8,128)S(1)}, s32[64,256]{1,0:T(8,128)}, u32[]{:S(2)}) copy-start(s32[64,256]{1,0:T(8,128)} %param.27) | copy-start | bytes 196612
  25.2 113.4 %copy-start.8 = (s32[256]{0:T(256)S(1)}, s32[256]{0:T(256)}, u32[]{:S(2)}) copy-start(s32[256]{0:T(256)} %param.26) | copy-start | bytes 3076
  25.2 113.4 %copy-start.9 = (f32[256]{0:T(256)S(1)}, f32[256]{0:T(256)}, u32[]{:S(2)}) copy-start(f32[256]{0:T(256)} %param.25) | copy-start | bytes 3076
  25.3 113.4 %copy-start.10 = (f32[256]{0:T(256)S(1)}, f32[256]{0:T(256)}, u32[]{:S(2)}) copy-start(f32[256]{0:T(256)} %param.24) | copy-start | bytes 3076
  25.3 115.4 %copy-start.5 = (s32[128]{0:T(128)S(1)}, s32[128]{0:T(128)}, u32[]{:S(2)}) copy-start(s32[128]{0:T(128)} %param.18) | copy-start | bytes 1540
  140.4 163.1 %reduce-scatter.9.cloned.1.call-start = ((), (), s32[]{:S(2)}) async-start(), calls=%async_computation.8 | async-start | bytes 2162688 | tf_op jit(solution)/shard_map/reduce_scatter | solution.py:95
  225.0 122.9 %all-gather.8.cloned.1.call-start = ((), (), s32[]{:S(2)}) async-start(), calls=%async_computation.9 | async-start | bytes 1081344 | tf_op jit(solution)/shard_map/all_gather | solution.py:106
  305.0 147.6 %reduce-scatter.11.cloned.1.call-start = ((), (), s32[]{:S(2)}) async-start(), calls=%async_computation.10 | async-start | bytes 2162688 | tf_op jit(solution)/shard_map/reduce_scatter | solution.py:95
  374.2 78.4 %copy-start.2 = (f32[64,2,128]{2,0,1:T(8,128)S(1)}, f32[64,2,128]{2,0,1:T(8,128)}, u32[]{:S(2)}) copy-start(f32[64,2,128]{2,0,1:T(8,128)} %reduce-scatter.7.cloned.1.call-done) | copy-start | bytes 196612
  374.2 122.9 %all-gather.10.cloned.1.call-start = ((), (), s32[]{:S(2)}) async-start(), calls=%async_computation.11 | async-start | bytes 1081344 | tf_op jit(solution)/shard_map/all_gather | solution.py:106
  454.1 147.9 %reduce-scatter.13.cloned.1.call-start = ((), (), s32[]{:S(2)}) async-start(), calls=%async_computation.12 | async-start | bytes 2162688 | tf_op jit(solution)/shard_map/reduce_scatter | solution.py:95
  523.5 78.4 %copy-start.3 = (f32[64,2,128]{2,0,1:T(8,128)S(1)}, f32[64,2,128]{2,0,1:T(8,128)}, u32[]{:S(2)}) copy-start(f32[64,2,128]{2,0,1:T(8,128)} %reduce-scatter.9.cloned.1.call-done) | copy-start | bytes 196612
  523.6 123.1 %all-gather.12.cloned.1.call-start = ((), (), s32[]{:S(2)}) async-start(), calls=%async_computation.13 | async-start | bytes 1081344 | tf_op jit(solution)/shard_map/all_gather | solution.py:106
  603.5 147.8 %reduce-scatter.15.cloned.1.call-start = ((), (), s32[]{:S(2)}) async-start(), calls=%async_computation.14 | async-start | bytes 2162688 | tf_op jit(solution)/shard_map/reduce_scatter | solution.py:95
  672.9 122.9 %all-gather.14.cloned.1.call-start = ((), (), s32[]{:S(2)}) async-start(), calls=%async_computation.15 | async-start | bytes 1081344 | tf_op jit(solution)/shard_map/all_gather | solution.py:106
  752.8 147.7 %reduce-scatter.17.cloned.1.call-start = ((), (), s32[]{:S(2)}) async-start(), calls=%async_computation.16 | async-start | bytes 2162688 | tf_op jit(solution)/shard_map/reduce_scatter | solution.py:95
  822.0 1.0 copy-start.1
  822.0 183.5 %all-reduce.3.cloned.1.call-start = ((), (), s32[]{:S(2)}) async-start(), calls=%async_computation.17 | async-start | bytes 262144 | tf_op jit(solution)/shard_map/psum | solution.py:112
  901.3 124.9 %copy-start.4 = (f32[64,256]{1,0:T(8,128)}, f32[64,256]{1,0:T(8,128)S(1)}, u32[]{:S(2)}) copy-start(f32[64,256]{1,0:T(8,128)S(1)} %copy_bitcast_fusion.1) | copy-start | bytes 196612
  (1 other events, 0.7 us)
Sparse Core Ops, SparseCore 0:
  23.5 80.7 reduce-scatter.6
  140.5 58.0 all-gather.5
  225.2 78.2 reduce-scatter.8
  306.1 41.7 all-gather.7
  374.3 78.2 reduce-scatter.10
  455.3 41.7 all-gather.9
  523.7 78.2 reduce-scatter.12
  604.8 41.7 all-gather.11
  673.0 78.2 reduce-scatter.14
  753.9 41.7 all-gather.13
  822.2 78.2 reduce-scatter.16
  904.1 101.3 all-reduce.2
where the time goes:
time: 1040 us; the launch traced here: 1030 us
  waiting for transfers between devices  722 us (69%)
  blocking collectives  127 us (12%)
  matrix products  103 us (10%)
  local copies, waits for them, and re-layouts  51.7 us (5%)
  between operations  15.5 us (1%)
  other arithmetic  13.9 us (1%)
    reduce_scatter x6, waiting for transfers between devices, body(): lax.psum_scatter(jnp.einsum('nt,rtf->rnf', dense_hot, pushed, precision=h...  390 us
    all_gather x5, waiting for transfers between devices, body(): every_firm = lax.all_gather(firm_round, 'tiles', axis=1, tiled=True)  230 us
    unnamed x1, blocking collectives  110 us
    psum x1, waiting for transfers between devices, body(): summed = lax.psum(local_term, 'tiles')  102 us
    dot_general x5, matrix products, body(): jnp.einsum('twf,rtf->rtw', tiles_w, tile_firm, preferred_element_type=jnp...  28.7 us
    dot_general x6, matrix products, body(): jnp.einsum('nt,rtf->rnf', dense_hot, pushed, precision=highest)  24.9 us
    dot_general x6, matrix products, body(): jnp.einsum('twf,rtw->rtf', tiles_w, tile_values, preferred_element_type=j...  24.6 us
  transfers between devices with their start and end apart: 12, of which 11 were waited for; matrix products, arithmetic and copies ran while one was open for 1% of the time, Pallas kernels for 0%

commit v1 on v0

--- a/solution.py
+++ b/solution.py
@@ -103,7 +103,10 @@
         firm_older, firm_newer = (firm_newer, firm_now)
         if sweep_index + 1 < SWEEPS:
             firm_round = firm_now.astype(jnp.bfloat16)
-            every_firm = lax.all_gather(firm_round, "tiles", axis=1, tiled=True)
+            every_firm = jnp.concatenate(
+                lax.all_to_all(jnp.stack([firm_round] * lax.axis_size("tiles")), "tiles", 0, 0),
+                axis=1,
+            )
             tile_firm = jnp.take(every_firm, tile_block, axis=1)
     worker_effect = worker_now.reshape(replicas_here, WORK_BLOCKS * tile_cells)
     firm_flat = firm_now.reshape(replicas_here, FIRM_BLOCKS * tile_cells)

time: 1040 us -> 935 us (0.90)
  waiting for transfers between devices: 722 us -> 506 us
  blocking collectives: 127 us -> 211 us
  starting transfers between devices: 0.68 us -> 23.4 us
    all_gather x5 -> x0, waiting for transfers between devices: 230 us -> none  [body(): every_firm = lax.all_gather(firm_round, 'tiles', axis=1, tiled=True)]
    all_to_all x0 -> x4, blocking collectives: none -> 84 us  [body(): lax.all_to_all(jnp.stack([firm_round] * lax.axis_size('tiles')), 'tiles',...]
    all_to_all x0 -> x1, starting transfers between devices: none -> 22.9 us  [body(): lax.all_to_all(jnp.stack([firm_round] * lax.axis_size('tiles')), 'tiles',...]
    all_to_all x0 -> x1, waiting for transfers between devices: none -> 14.7 us  [body(): lax.all_to_all(jnp.stack([firm_round] * lax.axis_size('tiles')), 'tiles',...]
  transfers between devices with their start and end apart: 12 -> 8, of which waited for: 11 -> 7; matrix products, arithmetic and copies ran while one was open for 1% -> 1% of each run, Pallas kernels for 0% -> 0%
where the time goes in v1:
time: 935 us; the launch traced here: 927 us
  waiting for transfers between devices  506 us (54%)
  blocking collectives  211 us (23%)
  matrix products  103 us (11%)
  local copies, waits for them, and re-layouts  57.4 us (6%)
  starting transfers between devices  23.4 us (3%)
  between operations  15.7 us (2%)
  other arithmetic  10.8 us (1%)
    reduce_scatter x6, waiting for transfers between devices, body(): lax.psum_scatter(jnp.einsum('nt,rtf->rnf', dense_hot, pushed, precision=h...  389 us
    unnamed x1, blocking collectives  110 us
    psum x1, waiting for transfers between devices, body(): summed = lax.psum(local_term, 'tiles')  102 us
    all_to_all x4, blocking collectives, body(): lax.all_to_all(jnp.stack([firm_round] * lax.axis_size('tiles')), 'tiles',...  84 us
    dot_general x5, matrix products, body(): jnp.einsum('twf,rtf->rtw', tiles_w, tile_firm, preferred_element_type=jnp...  28.8 us
    transpose x6, local copies, waits for them, and re-layouts, body(): jnp.einsum('nt,rtf->rnf', dense_hot, pushed, precision=highest)  26.2 us
    dot_general x6, matrix products, body(): jnp.einsum('nt,rtf->rnf', dense_hot, pushed, precision=highest)  24.9 us
    dot_general x6, matrix products, body(): jnp.einsum('twf,rtw->rtf', tiles_w, tile_values, preferred_element_type=j...  24.6 us
  transfers between devices with their start and end apart: 8, of which 7 were waited for; matrix products, arithmetic and copies ran while one was open for 1% of the time, Pallas kernels for 0%

profile of v1, /device:TPU:6, one launch (start us, length us, event | category | flops | bytes accessed | tf_op | source)
XLA Modules:
  0.0 926.9 jit_solution(12816127627307912274)
XLA Ops:
  16.6 4.2 fusion.56
  28.9 109.8 %all-reduce = f32[64,128]{1,0:T(8,128)S(1)} all-reduce(f32[64,128]{1,0:T(8,128)S(1)} %fusion.164), channel_id=3, replica_groups=mesh['tiles'=32,'reps'=4] {'tiles'}, use_global_device_ids=true, to_apply=%region_3.0.clone | all-reduce | flops 8192 | bytes 65536
  141.0 22.9 %all-to-all-start = ((bf16[32,64,2,128]{3,1,2,0:T(8,128)(2,1)}), bf16[32,64,2,128]{3,1,2,0:T(8,128)(2,1)S(1)}, u32[]{:S(2)}, u32[]{:S(2)}) async-start(bf16[32,64,2,128]{3,1,2,0:T(8,128)(2,1)} %stack.10), calls=%async_computation.1 | async-start | bytes 2097152 | tf_op jit(solution)/shard_map/all_to_all | solution.py:107
  164.4 14.7 %all-to-all-done = bf16[32,64,2,128]{3,1,2,0:T(8,128)(2,1)S(1)} async-done(((bf16[32,64,2,128]{3,1,2,0:T(8,128)(2,1)}), bf16[32,64,2,128]{3,1,2,0:T(8,128)(2,1)S(1)}, u32[]{:S(2)}, u32[]{:S(2)}) %all-to-all-start) | async-done | bytes 1048608 | tf_op jit(solution)/shard_map/all_to_all | solution.py:107
  181.2 5.8 convolution_bitcast_fusion.9
  201.3 12.4 %copy.94 = f32[64,64,128]{2,0,1:T(8,128)} copy(f32[64,64,128]{2,1,0:T(8,128)S(1)} %fusion.59) | data formatting | bytes 4194304 | tf_op jit(solution)/shard_map/nt,rtf->rnf/transpose | solution.py:96
  213.8 79.1 %reduce-scatter.9.cloned.1.call-done = f32[64,2,128]{2,0,1:T(8,128)} async-done(((f32[64,64,128]{2,0,1:T(8,128)}), f32[64,2,128]{2,0,1:T(8,128)}) %reduce-scatter.9.cloned.1.call-update) | async-done | bytes 65552 | tf_op jit(solution)/shard_map/reduce_scatter | solution.py:95
  294.0 21.0 %all_to_all.25 = bf16[32,64,2,128]{3,1,2,0:T(8,128)(2,1)S(1)} all-to-all(bf16[32,64,2,128]{3,1,2,0:T(8,128)(2,1)S(1)} %stack.11), channel_id=1, replica_groups=mesh['tiles'=32,'reps'=4] {'tiles'}, dimensions={0} | all-to-all | bytes 2097152 | tf_op jit(solution)/shard_map/all_to_all | solution.py:107
  317.1 5.8 convolution_bitcast_fusion.7
  333.0 4.2 fusion.62
  340.2 78.0 %reduce-scatter.11.cloned.1.call-done = f32[64,2,128]{2,0,1:T(8,128)} async-done(((f32[64,64,128]{2,0,1:T(8,128)}), f32[64,2,128]{2,0,1:T(8,128)}) %reduce-scatter.11.cloned.1.call-update) | async-done | bytes 65552 | tf_op jit(solution)/shard_map/reduce_scatter | solution.py:95
  419.3 21.0 %all_to_all.26 = bf16[32,64,2,128]{3,1,2,0:T(8,128)(2,1)S(1)} all-to-all(bf16[32,64,2,128]{3,1,2,0:T(8,128)(2,1)S(1)} %stack.12), channel_id=1, replica_groups=mesh['tiles'=32,'reps'=4] {'tiles'}, dimensions={0} | all-to-all | bytes 2097152 | tf_op jit(solution)/shard_map/all_to_all | solution.py:107
  442.5 5.8 convolution_bitcast_fusion.5
  458.4 4.2 fusion.65
  465.4 78.0 %reduce-scatter.13.cloned.1.call-done = f32[64,2,128]{2,0,1:T(8,128)} async-done(((f32[64,64,128]{2,0,1:T(8,128)}), f32[64,2,128]{2,0,1:T(8,128)}) %reduce-scatter.13.cloned.1.call-update) | async-done | bytes 65552 | tf_op jit(solution)/shard_map/reduce_scatter | solution.py:95
  544.4 21.0 %all_to_all.27 = bf16[32,64,2,128]{3,1,2,0:T(8,128)(2,1)S(1)} all-to-all(bf16[32,64,2,128]{3,1,2,0:T(8,128)(2,1)S(1)} %stack.13), channel_id=1, replica_groups=mesh['tiles'=32,'reps'=4] {'tiles'}, dimensions={0} | all-to-all | bytes 2097152 | tf_op jit(solution)/shard_map/all_to_all | solution.py:107
  567.6 5.8 convolution_bitcast_fusion.3
  590.5 77.9 %reduce-scatter.15.cloned.1.call-done = f32[64,2,128]{2,0,1:T(8,128)} async-done(((f32[64,64,128]{2,0,1:T(8,128)}), f32[64,2,128]{2,0,1:T(8,128)}) %reduce-scatter.15.cloned.1.call-update) | async-done | bytes 65552 | tf_op jit(solution)/shard_map/reduce_scatter | solution.py:95
  669.6 21.0 %all_to_all.28 = bf16[32,64,2,128]{3,1,2,0:T(8,128)(2,1)S(1)} all-to-all(bf16[32,64,2,128]{3,1,2,0:T(8,128)(2,1)S(1)} %stack.14), channel_id=1, replica_groups=mesh['tiles'=32,'reps'=4] {'tiles'}, dimensions={0} | all-to-all | bytes 2097152 | tf_op jit(solution)/shard_map/all_to_all | solution.py:107
  692.7 5.8 convolution_bitcast_fusion.1
  708.7 4.2 fusion.71
  717.7 75.9 %reduce-scatter.17.cloned.1.call-done = f32[64,2,128]{2,0,1:T(8,128)} async-done(((f32[64,64,128]{2,0,1:T(8,128)}), f32[64,2,128]{2,0,1:T(8,128)}) %reduce-scatter.17.cloned.1.call-update) | async-done | bytes 65552 | tf_op jit(solution)/shard_map/reduce_scatter | solution.py:95
  796.6 102.3 %all-reduce.3.cloned.1.call-done = f32[64,512]{1,0:T(8,128)} async-done(((f32[64,512]{1,0:T(8,128)}), f32[64,512]{1,0:T(8,128)}) %all-reduce.3.cloned.1.call-update) | async-done | bytes 131088 | tf_op jit(solution)/shard_map/psum | solution.py:115
  900.2 17.3 %psum.15 = f32[16,512]{1,0:T(8,128)S(1)} all-reduce(f32[16,512]{1,0:T(8,128)S(1)} %fusion.162), channel_id=1, replica_groups=mesh['tiles'=32,'reps'=4] {'reps'}, use_global_device_ids=true, to_apply=%region_11.14 | all-reduce | flops 8192 | bytes 65536 | tf_op jit(solution)/shard_map/psum | solution.py:121
  (109 shorter events, 113.8 us)
Async XLA Ops:
  7.2 708.6 %copy-start = (f32[512,512]{1,0:T(8,128)S(1)}, f32[512,512]{1,0:T(8,128)}, u32[]{:S(2)}) copy-start(f32[512,512]{1,0:T(8,128)} %param.29) | copy-start | bytes 3145732
  7.2 3.1 copy-start.11
  7.2 3.1 copy-start.6
  7.2 131.7 %reduce-scatter.7.cloned.1.call-start = ((), (), s32[]{:S(2)}) async-start(), calls=%async_computation.11 | async-start | bytes 2162688 | tf_op jit(solution)/shard_map/reduce_scatter | solution.py:95
  23.3 0.7 copy-start.12
  25.2 113.4 %copy-start.7 = (s32[64,256]{1,0:T(8,128)S(1)}, s32[64,256]{1,0:T(8,128)}, u32[]{:S(2)}) copy-start(s32[64,256]{1,0:T(8,128)} %param.27) | copy-start | bytes 196612
  25.2 113.4 %copy-start.8 = (s32[256]{0:T(256)S(1)}, s32[256]{0:T(256)}, u32[]{:S(2)}) copy-start(s32[256]{0:T(256)} %param.26) | copy-start | bytes 3076
  25.3 113.4 %copy-start.9 = (f32[256]{0:T(256)S(1)}, f32[256]{0:T(256)}, u32[]{:S(2)}) copy-start(f32[256]{0:T(256)} %param.25) | copy-start | bytes 3076
  25.3 113.4 %copy-start.10 = (f32[256]{0:T(256)S(1)}, f32[256]{0:T(256)}, u32[]{:S(2)}) copy-start(f32[256]{0:T(256)} %param.24) | copy-start | bytes 3076
  28.7 135.5 %copy-start.5 = (s32[128]{0:T(128)S(1)}, s32[128]{0:T(128)}, u32[]{:S(2)}) copy-start(s32[128]{0:T(128)} %param.18) | copy-start | bytes 1540
  141.0 38.1 %all-to-all-start = ((bf16[32,64,2,128]{3,1,2,0:T(8,128)(2,1)}), bf16[32,64,2,128]{3,1,2,0:T(8,128)(2,1)S(1)}, u32[]{:S(2)}, u32[]{:S(2)}) async-start(bf16[32,64,2,128]{3,1,2,0:T(8,128)(2,1)} %stack.10), calls=%async_computation.1 | async-start | bytes 2097152 | tf_op jit(solution)/shard_map/all_to_all | solution.py:107
  163.9 129.0 %reduce-scatter.9.cloned.1.call-start = ((), (), s32[]{:S(2)}) async-start(), calls=%async_computation.12 | async-start | bytes 2162688 | tf_op jit(solution)/shard_map/reduce_scatter | solution.py:95
  213.7 204.5 %reduce-scatter.11.cloned.1.call-start = ((), (), s32[]{:S(2)}) async-start(), calls=%async_computation.13 | async-start | bytes 2162688 | tf_op jit(solution)/shard_map/reduce_scatter | solution.py:95
  340.2 78.0 %copy-start.2 = (f32[64,2,128]{2,0,1:T(8,128)S(1)}, f32[64,2,128]{2,0,1:T(8,128)}, u32[]{:S(2)}) copy-start(f32[64,2,128]{2,0,1:T(8,128)} %reduce-scatter.7.cloned.1.call-done) | copy-start | bytes 196612
  340.2 203.1 %reduce-scatter.13.cloned.1.call-start = ((), (), s32[]{:S(2)}) async-start(), calls=%async_computation.14 | async-start | bytes 2162688 | tf_op jit(solution)/shard_map/reduce_scatter | solution.py:95
  465.3 78.0 %copy-start.3 = (f32[64,2,128]{2,0,1:T(8,128)S(1)}, f32[64,2,128]{2,0,1:T(8,128)}, u32[]{:S(2)}) copy-start(f32[64,2,128]{2,0,1:T(8,128)} %reduce-scatter.9.cloned.1.call-done) | copy-start | bytes 196612
  465.3 203.2 %reduce-scatter.15.cloned.1.call-start = ((), (), s32[]{:S(2)}) async-start(), calls=%async_computation.15 | async-start | bytes 2162688 | tf_op jit(solution)/shard_map/reduce_scatter | solution.py:95
  590.5 203.2 %reduce-scatter.17.cloned.1.call-start = ((), (), s32[]{:S(2)}) async-start(), calls=%async_computation.16 | async-start | bytes 2162688 | tf_op jit(solution)/shard_map/reduce_scatter | solution.py:95
  715.6 1.0 copy-start.1
  715.7 183.2 %all-reduce.3.cloned.1.call-start = ((), (), s32[]{:S(2)}) async-start(), calls=%async_computation.17 | async-start | bytes 262144 | tf_op jit(solution)/shard_map/psum | solution.py:115
  794.6 125.1 %copy-start.4 = (f32[64,256]{1,0:T(8,128)}, f32[64,256]{1,0:T(8,128)S(1)}, u32[]{:S(2)}) copy-start(f32[64,256]{1,0:T(8,128)S(1)} %copy_bitcast_fusion.1) | copy-start | bytes 196612
Sparse Core Ops, SparseCore 0:
  23.5 80.8 reduce-scatter.6
  213.9 78.9 reduce-scatter.8
  340.3 77.8 reduce-scatter.10
  465.4 77.8 reduce-scatter.12
  590.6 77.8 reduce-scatter.14
  715.8 77.8 reduce-scatter.16
  797.5 101.3 all-reduce.2
